TPU v7x, 32 devices: a whole 2x2x4 slice. The times are simulated.
32 devices in a mesh: replica: 8 (over z, y), model: 4 (over x, core).
Axes of the slice: x: 2, y: 2, z: 4, core: 2. Of those that a mesh axis runs over, the one named last changes fastest.
Arguments:
- partial_up: float32 [8, 1024, 4096], P('replica', None, 'model'), may hold values from -4 to 4
- partial_down: float32 [8, 4096, 1024], P('replica', 'model'), may hold values from -4 to 4
- partial_norm: float32 [8, 1024], P('replica'), may hold values from -8 to 8
- partial_bias: float32 [8, 1024], P('replica'), may hold values from -8 to 8
- master_up: float32 [1024, 4096], P('replica', 'model'), may hold values from -0.1875 to 0.1875
- master_down: float32 [4096, 1024], P('model', 'replica'), may hold values from -0.09375 to 0.09375
- master_norm: float32 [1024], P('replica'), may hold values from 0.25 to 1.75
- master_bias: float32 [1024], P('replica'), may hold values from -3 to 3
- memory_up: float32 [1024, 4096], P('replica', 'model'), may hold values from 0.05 to 0.8
- memory_down: float32 [4096, 1024], P('model', 'replica'), may hold values from 0.05 to 0.8
- memory_norm: float32 [1024], P('replica'), may hold values from 0.05 to 0.8
- memory_bias: float32 [1024], P('replica'), may hold values from 0.05 to 0.8
Outputs:
- compute_up: bfloat16 [1024, 4096], P(None, 'model')
- compute_down: bfloat16 [4096, 1024], P('model')
- compute_norm: bfloat16 [1024], replicated
- compute_bias: bfloat16 [1024], replicated
- stepped_up: float32 [1024, 4096], P('replica', 'model')
- stepped_down: float32 [4096, 1024], P('model', 'replica')
- stepped_norm: float32 [1024], P('replica')
- stepped_bias: float32 [1024], P('replica')
- state_new_up: float32 [1024, 4096], P('replica', 'model')
- state_new_down: float32 [4096, 1024], P('model', 'replica')
- state_new_norm: float32 [1024], P('replica')
- state_new_bias: float32 [1024], P('replica')
All inputs are finite; a program needn't handle non-finite values.
Results may differ from a plain program's by a relative error of at most 0.001.
Values may be sent and summed in bfloat16 or wider, within the bound.
A program may use at most 128 MiB of HBM per device.

v0:
```python
import jax
import jax.numpy as jnp
from jax import lax
from jax.sharding import PartitionSpec as P

learn_rate = 0.05
hold_rate = 0.9


def on_device(
    partial_up,
    partial_down,
    partial_norm,
    partial_bias,
    master_up,
    master_down,
    master_norm,
    master_bias,
    memory_up,
    memory_down,
    memory_norm,
    memory_bias,
):
    mean_up, mean_down = (
        lax.psum_scatter(partial_up[0], "replica", scatter_dimension=0, tiled=True),
        lax.psum_scatter(partial_down[0], "replica", scatter_dimension=1, tiled=True),
    )
    whole_norm, whole_bias = lax.psum((partial_norm[0], partial_bias[0]), "replica")
    place = lax.axis_index("replica")
    mean_norm = lax.dynamic_slice_in_dim(
        whole_norm, place * master_norm.shape[0], master_norm.shape[0]
    )
    mean_bias = lax.dynamic_slice_in_dim(
        whole_bias, place * master_bias.shape[0], master_bias.shape[0]
    )
    mean_rate = lax.axis_size("replica") ** (-0.5)
    mean_up = mean_up * mean_rate
    mean_down = mean_down * mean_rate
    mean_norm = mean_norm * mean_rate
    mean_bias = mean_bias * mean_rate
    state_new_up = hold_rate * memory_up + (1.0 - hold_rate) * mean_up * mean_up
    stepped_up = master_up - learn_rate * mean_up * lax.rsqrt(state_new_up + 1e-06)
    state_new_down = hold_rate * memory_down + (1.0 - hold_rate) * mean_down * mean_down
    stepped_down = master_down - learn_rate * mean_down * lax.rsqrt(state_new_down + 1e-06)
    state_new_norm = hold_rate * memory_norm + (1.0 - hold_rate) * mean_norm * mean_norm
    stepped_norm = master_norm - learn_rate * mean_norm * lax.rsqrt(state_new_norm + 1e-06)
    state_new_bias = hold_rate * memory_bias + (1.0 - hold_rate) * mean_bias * mean_bias
    stepped_bias = master_bias - learn_rate * mean_bias * lax.rsqrt(state_new_bias + 1e-06)
    compute_up, compute_down, compute_norm, compute_bias = (
        lax.all_gather(stepped_up.astype(jnp.bfloat16), "replica", axis=0, tiled=True),
        lax.all_gather(stepped_down.astype(jnp.bfloat16), "replica", axis=1, tiled=True),
        lax.all_gather(stepped_norm.astype(jnp.bfloat16), "replica", axis=0, tiled=True),
        lax.all_gather(stepped_bias.astype(jnp.bfloat16), "replica", axis=0, tiled=True),
    )
    return (
        compute_up,
        compute_down,
        compute_norm,
        compute_bias,
        stepped_up,
        stepped_down,
        stepped_norm,
        stepped_bias,
        state_new_up,
        state_new_down,
        state_new_norm,
        state_new_bias,
    )


def solution(mesh):
    in_specs = (
        P("replica", None, "model"),
        P("replica", "model", None),
        P("replica", None),
        P("replica", None),
        P("replica", "model"),
        P("model", "replica"),
        P("replica"),
        P("replica"),
        P("replica", "model"),
        P("model", "replica"),
        P("replica"),
        P("replica"),
    )
    out_specs = (
        P(None, "model"),
        P("model", None),
        P(),
        P(),
        P("replica", "model"),
        P("model", "replica"),
        P("replica"),
        P("replica"),
        P("replica", "model"),
        P("model", "replica"),
        P("replica"),
        P("replica"),
    )
    return jax.shard_map(
        on_device, mesh=mesh, in_specs=in_specs, out_specs=out_specs, check_vma=False
    )
```

profile of v0, /device:TPU:0, one launch (start us, length us, event | category | flops | bytes accessed | tf_op | source)
XLA Modules:
  0.0 309.0 jit_solution(2177770906514875568)
XLA Ops:
  7.2 0.0 reduce-scatter.3.cloned.1.call-start
  7.2 0.7 reduce-scatter.3.cloned.1.call-update
  7.9 0.0 reduce-scatter.5.cloned.1.call-start
  8.0 0.0 copy-start.1
  8.0 0.0 copy-start.2
  8.0 0.7 reduce-scatter.5.cloned.1.call-update
  8.7 0.0 copy-start.3
  8.7 0.0 copy-start.4
  8.7 0.0 all-gather.5.cloned.1.call-start
  8.7 93.9 %reduce-scatter.3.cloned.1.call-done = f32[128,1024]{1,0:T(8,128)} async-done(((f32[1024,1024]{1,0:T(8,128)}), f32[128,1024]{1,0:T(8,128)}) %reduce-scatter.3.cloned.1.call-update) | async-done | bytes 524304 | tf_op jit(solution)/shard_map/reduce_scatter | solution.py:25
  102.7 0.0 copy-done.1
  102.7 0.0 copy-done.2
  102.7 2.3 fusion.1
  104.9 0.0 copy-start.5
  105.0 0.0 copy-start.6
  105.0 0.0 copy-start.7
  105.0 0.0 copy-start.8
  105.0 0.0 copy-start.9
  105.0 0.0 copy-start.10
  105.0 0.0 all-gather.5.cloned.1.call-update
  105.0 0.0 all-gather.7.cloned.1.call-start
  105.1 89.6 %reduce-scatter.5.cloned.1.call-done = f32[1024,128]{1,0:T(8,128)} async-done(((f32[1024,1024]{1,0:T(8,128)}), f32[1024,128]{1,0:T(8,128)}) %reduce-scatter.5.cloned.1.call-update) | async-done | bytes 524304 | tf_op jit(solution)/shard_map/reduce_scatter | solution.py:26
  194.6 0.0 copy-done.3
  194.7 0.0 copy-done.4
  194.7 2.3 fusion
  196.9 0.0 all-gather.7.cloned.1.call-update
  197.0 0.0 copy-done.5
  197.0 0.0 copy-done.6
  197.0 20.6 %all-reduce = (f32[1024]{0:T(1024)S(1)}, f32[1024]{0:T(1024)S(1)}) all-reduce(f32[1024]{0:T(1024)S(1)} %bitcast.12, f32[1024]{0:T(1024)S(1)} %bitcast.13), channel_id=1, replica_groups=mesh['replica'=8,'model'=4] {'replica'}, use_global_device_ids=true, to_apply=%region_2.0 | all-reduce | flops 2048 | bytes 16384 | tf_op jit(solution)/shard_map/psum | solution.py:28
  217.6 0.0 copy-done.7
  217.6 0.0 copy-done.8
  217.7 0.6 convert_bitcast_fusion.1
  218.3 16.6 %all-gather = bf16[8,1,128]{2,1,0:T(2,128)(2,1)S(1)} all-gather(bf16[1,1,128]{2,1,0:T(2,128)(2,1)S(1)} %get-tuple-element.17), channel_id=1, replica_groups=mesh['replica'=8,'model'=4] {'replica'}, dimensions={0}, use_global_device_ids=true | all-gather | bytes 2304 | tf_op jit(solution)/shard_map/all_gather | solution.py:52
  234.8 0.6 reduce
  235.4 0.0 copy-done.9
  235.4 0.0 copy-done.10
  235.4 0.6 convert_bitcast_fusion
  236.0 18.6 %all-gather.1 = bf16[8,1,128]{2,1,0:T(2,128)(2,1)S(1)} all-gather(bf16[1,1,128]{2,1,0:T(2,128)(2,1)S(1)} %get-tuple-element.14), channel_id=1, replica_groups=mesh['replica'=8,'model'=4] {'replica'}, dimensions={0}, use_global_device_ids=true | all-gather | bytes 2304 | tf_op jit(solution)/shard_map/all_gather | solution.py:53
  254.6 0.6 reduce.1
  255.2 0.0 all-gather.5.cloned.1.call-done
  255.2 42.8 %all-gather.7.cloned.1.call-done = bf16[1024,1024]{1,0:T(8,128)(2,1)} async-done(((bf16[1024,128]{1,0:T(8,128)(2,1)}), bf16[1024,1024]{1,0:T(8,128)(2,1)}) %all-gather.7.cloned.1.call-update) | async-done | bytes 2097168 | tf_op jit(solution)/shard_map/all_gather | solution.py:51
  297.9 0.0 copy-start
  297.9 3.2 %copy.26 = bf16[1024,1024]{1,0:T(8,128)(2,1)} copy(bf16[1024,1024]{1,0:T(8,128)(2,1)} %all-gather.5.cloned.1.call-done) | data formatting | bytes 4194304
  301.2 0.0 copy-done
  301.2 1.3 copy.27
Async XLA Ops:
  7.2 95.5 %reduce-scatter.3.cloned.1.call-start = ((), (), s32[]{:S(2)}) async-start(), calls=%async_computation.2 | async-start | bytes 4718592 | tf_op jit(solution)/shard_map/reduce_scatter | solution.py:25
  7.9 186.7 %reduce-scatter.5.cloned.1.call-start = ((), (), s32[]{:S(2)}) async-start(), calls=%async_computation.4 | async-start | bytes 4718592 | tf_op jit(solution)/shard_map/reduce_scatter | solution.py:26
  8.0 94.7 %copy-start.1 = (f32[128,1024]{1,0:T(8,128)S(1)}, f32[128,1024]{1,0:T(8,128)}, u32[]{:S(2)}) copy-start(f32[128,1024]{1,0:T(8,128)} %param.16) | copy-start | bytes 1572868
  8.0 94.7 %copy-start.2 = (f32[128,1024]{1,0:T(8,128)S(1)}, f32[128,1024]{1,0:T(8,128)}, u32[]{:S(2)}) copy-start(f32[128,1024]{1,0:T(8,128)} %param.20) | copy-start | bytes 1572868
  8.7 186.0 %copy-start.3 = (f32[1024,128]{1,0:T(8,128)S(1)}, f32[1024,128]{1,0:T(8,128)}, u32[]{:S(2)}) copy-start(f32[1024,128]{1,0:T(8,128)} %param.17) | copy-start | bytes 1572868
  8.7 186.0 %copy-start.4 = (f32[1024,128]{1,0:T(8,128)S(1)}, f32[1024,128]{1,0:T(8,128)}, u32[]{:S(2)}) copy-start(f32[1024,128]{1,0:T(8,128)} %param.21) | copy-start | bytes 1572868
  8.7 246.5 %all-gather.5.cloned.1.call-start = ((), (), s32[]{:S(2)}) async-start(), calls=%async_computation.3 | async-start | bytes 2359296 | tf_op jit(solution)/shard_map/all_gather | solution.py:50
  104.9 92.0 %copy-start.5 = (f32[1,1024]{1,0:T(1,128)S(1)}, f32[1,1024]{1,0:T(1,128)}, u32[]{:S(2)}) copy-start(f32[1,1024]{1,0:T(1,128)} %param.14) | copy-start | bytes 12292
  105.0 92.0 %copy-start.6 = (f32[1,1024]{1,0:T(1,128)S(1)}, f32[1,1024]{1,0:T(1,128)}, u32[]{:S(2)}) copy-start(f32[1,1024]{1,0:T(1,128)} %param.15) | copy-start | bytes 12292
  105.0 112.7 %copy-start.7 = (f32[128]{0:T(128)S(1)}, f32[128]{0:T(128)}, u32[]{:S(2)}) copy-start(f32[128]{0:T(128)} %param.18) | copy-start | bytes 1540
  105.0 112.7 %copy-start.8 = (f32[128]{0:T(128)S(1)}, f32[128]{0:T(128)}, u32[]{:S(2)}) copy-start(f32[128]{0:T(128)} %param.22) | copy-start | bytes 1540
  105.0 130.4 %copy-start.9 = (f32[128]{0:T(128)S(1)}, f32[128]{0:T(128)}, u32[]{:S(2)}) copy-start(f32[128]{0:T(128)} %param.19) | copy-start | bytes 1540
  105.0 130.4 %copy-start.10 = (f32[128]{0:T(128)S(1)}, f32[128]{0:T(128)}, u32[]{:S(2)}) copy-start(f32[128]{0:T(128)} %param.23) | copy-start | bytes 1540
  105.0 192.9 %all-gather.7.cloned.1.call-start = ((), (), s32[]{:S(2)}) async-start(), calls=%async_computation.5 | async-start | bytes 2359296 | tf_op jit(solution)/shard_map/all_gather | solution.py:51
  297.9 3.2 %copy-start = (bf16[1024,1024]{1,0:T(8,128)(2,1)S(1)}, bf16[1024,1024]{1,0:T(8,128)(2,1)}, u32[]{:S(2)}) copy-start(bf16[1024,1024]{1,0:T(8,128)(2,1)} %all-gather.7.cloned.1.call-done) | copy-start | bytes 6291460
Sparse Core Ops, SparseCore 0:
  11.6 91.0 reduce-scatter.2
  106.3 88.3 reduce-scatter.4
  197.4 49.1 all-gather.4
  249.0 48.8 all-gather.6
where the time goes:
time: 309 us
  waiting for transfers between devices  228 us (74%)
  blocking collectives  55.8 us (18%)
  between operations  13.9 us (4%)
  other arithmetic  6.94 us (2%)
  local copies, waits for them, and re-layouts  4.6 us (1%)
    reduce_scatter x1, waiting for transfers between devices, on_device(): lax.psum_scatter(partial_up[0], 'replica', scatter_dimension=0, tiled=True)  93.9 us
    reduce_scatter x1, waiting for transfers between devices, on_device(): lax.psum_scatter(partial_down[0], 'replica', scatter_dimension=1, tiled=T...  89.6 us
    all_gather x1, waiting for transfers between devices, on_device(): lax.all_gather(stepped_down.astype(jnp.bfloat16), 'replica', axis=1, tile...  42.8 us
    psum x1, blocking collectives, on_device(): lax.psum((partial_norm[0], partial_bias[0]), 'replica')  20.6 us
    all_gather x1, blocking collectives, on_device(): lax.all_gather(stepped_bias.astype(jnp.bfloat16), 'replica', axis=0, tile...  18.6 us
    all_gather x1, blocking collectives, on_device(): lax.all_gather(stepped_norm.astype(jnp.bfloat16), 'replica', axis=0, tile...  16.6 us
  transfers between devices with their start and end apart: 4, of which 3 were waited for; matrix products, arithmetic and copies ran while one was open for 2% of the time, Pallas kernels for 0%

commit v1 on v0

--- a/solution.py
+++ b/solution.py
@@ -1,13 +1,18 @@
+import functools
+import math
+
 import jax
 import jax.numpy as jnp
 from jax import lax
+from jax.experimental import pallas as pl
+from jax.experimental.pallas import tpu as pltpu
 from jax.sharding import PartitionSpec as P
 
 learn_rate = 0.05
 hold_rate = 0.9
 
 
-def on_device(
+def plain(
     partial_up,
     partial_down,
     partial_norm,
@@ -68,6 +73,321 @@
     )
 
 
+CHUNKS = 4
+STEEP = 32.0
+SPAN = 124.0
+POWER = 2.0 * SPAN / math.log1p(STEEP)
+
+
+def encode(x, reach):
+    y = jnp.exp2(POWER * jnp.log(1.0 + jnp.abs(x) * (STEEP / reach)) - SPAN)
+    return jnp.where(x < 0.0, -y, y).astype(jnp.bfloat16)
+
+
+def decode(code, reach):
+    y = code.astype(jnp.float32)
+    grown = jnp.exp2((jnp.log(jnp.abs(y)) * (1.0 / math.log(2.0)) + SPAN) * (math.log1p(STEEP) / (2.0 * SPAN * math.log(2.0))))
+    x = (grown - 1.0) * (reach / STEEP)
+    return jnp.where(y < 0.0, -x, x)
+
+
+def update(total, master, memory, rate):
+    mean = total * rate
+    state = hold_rate * memory + (1.0 - hold_rate) * mean * mean
+    return master - learn_rate * mean * lax.rsqrt(state + 1e-06), state
+
+
+def kernel(
+    n,
+    pu, pd, mu, md, su, sd, pn, pb, mn, mb, sn, sb,
+    cu, cd, tu, td, vu, vd, cn, cb, tn, tb, vn, vb,
+    xu, xd, wu, wd, hu, hd, ou, od, qu, qd,
+    au, ad, ru, rd, bu, bd, zu, zd, gu, gd,
+    mine, theirs, step_s, state_s,
+    sem_in, sem_par, sem_as, sem_ar, sem_bs, sem_br, sem_ds, sem_dr, sem_es, sem_er,
+    sem_vs, sem_vr, sem_o, sem_cu, sem_cd,
+):
+    K = CHUNKS
+    nz = n // 2
+    me = lax.axis_index("replica")
+    y = lax.rem(me, 2)
+    z = lax.div(me, 2)
+    other = me + 1 - 2 * y
+    rate = n ** (-0.5)
+    reach = n / 2.0
+    wide = 128
+    hr = xu.shape[1] // K
+    rr = xd.shape[0] // K
+
+    def up_z(d):
+        return lax.rem(z + d, nz)
+
+    def from_z(d):
+        return lax.rem(z + nz - d, nz)
+
+    def remote(src, dst, ss, rs, who):
+        return pltpu.make_async_remote_copy(
+            src_ref=src, dst_ref=dst, send_sem=ss, recv_sem=rs,
+            device_id={"replica": who}, device_id_type=pl.DeviceIdType.MESH,
+        )
+
+    def rows(k, h):
+        return pl.ds(pl.multiple_of(k * h, h), h)
+
+    def lanes(b):
+        return pl.ds(pl.multiple_of(b * wide, wide), wide)
+
+    def load_in(m, k):
+        if m == 0:
+            return pltpu.make_async_copy(pu.at[:, rows(k, hr), :], xu.at[:, rows(k, hr), :], sem_in.at[m, k])
+        return pltpu.make_async_copy(pd.at[rows(k, rr), :], xd.at[rows(k, rr), :], sem_in.at[m, k])
+
+    def block(m, k, b):
+        if m == 0:
+            return xu[b, rows(k, hr), :]
+        return xd[rows(k, rr), lanes(b)]
+
+    def span(m, k):
+        return rows(k, (hr, rr)[m])
+
+    asend, arecv, bsend, brecv, gath = (au, ad), (ru, rd), (bu, bd), (zu, zd), (gu, gd)
+
+    def copy_a(m, k):
+        return remote(asend[m].at[k], arecv[m].at[k], sem_as.at[m, k], sem_ar.at[m, k], other)
+
+    def copy_b(m, k, d):
+        return remote(
+            bsend[m].at[k, up_z(d)], brecv[m].at[k, d - 1],
+            sem_bs.at[m, k, d - 1], sem_br.at[m, k, d - 1], 2 * up_z(d) + y,
+        )
+
+    def copy_d(m, k, d):
+        piece = gath[m].at[me, span(m, k), :]
+        return remote(piece, piece, sem_ds.at[m, k, d - 1], sem_dr.at[m, k, d - 1], 2 * up_z(d) + y)
+
+    def copy_e(m, k, d):
+        piece = gath[m].at[2 * from_z(d) + y, span(m, k), :]
+        return remote(piece, piece, sem_es.at[m, k, d], sem_er.at[m, k, d], other)
+
+    def copy_v(d):
+        return remote(mine, theirs.at[d - 1], sem_vs.at[d - 1], sem_vr.at[d - 1], lax.rem(me + d, n))
+
+    def copy_out(m, k, j):
+        src = ((ou, od), (qu, qd))[j][m]
+        dst = ((tu, td), (vu, vd))[j][m]
+        return pltpu.make_async_copy(src.at[span(m, k), :], dst.at[span(m, k), :], sem_o.at[m, k, j])
+
+    def copy_cu(k):
+        return pltpu.make_async_copy(gu.at[:, rows(k, hr), :], cu.at[:, rows(k, hr), :], sem_cu.at[k])
+
+    def copy_cd(k, b):
+        return pltpu.make_async_copy(gd.at[b, rows(k, rr), :], cd.at[rows(k, rr), lanes(b)], sem_cd.at[k, b])
+
+    def each(m, body):
+        lax.fori_loop(0, K, lambda k, c: (body(m, k), c)[1], 0)
+
+    params = [
+        pltpu.make_async_copy(a, b, sem_par.at[i])
+        for i, (a, b) in enumerate(((mu, wu), (md, wd), (su, hu), (sd, hd)))
+    ]
+    each(0, lambda m, k: load_in(m, k).start())
+    each(1, lambda m, k: load_in(m, k).start())
+    for p in params:
+        p.start()
+
+    mine[0:n, :] = pn[...]
+    mine[n : 2 * n, :] = pb[...]
+    for i, a in enumerate((mn, mb, sn, sb)):
+        mine[2 * n + i : 2 * n + i + 1, :] = a[...]
+    mine[2 * n + 4 : 2 * n + 8, :] = jnp.zeros((4, wide), jnp.float32)
+
+    barrier = pltpu.get_barrier_semaphore()
+    for d in range(1, n):
+        pl.semaphore_signal(
+            barrier, inc=1, device_id={"replica": lax.rem(me + d, n)},
+            device_id_type=pl.DeviceIdType.MESH,
+        )
+
+    def encode_a(m, k):
+        load_in(m, k).wait()
+
+        def one(t, c):
+            asend[m][k, t] = encode(block(m, k, 2 * t + 1 - y), reach)
+            return c
+
+        lax.fori_loop(0, nz, one, 0)
+
+    def phase_a(m, k):
+        encode_a(m, k)
+        copy_a(m, k).start()
+
+    def phase_b(m, k):
+        copy_a(m, k).wait_recv()
+
+        def one(t, c):
+            pair = block(m, k, 2 * t + y) + decode(arecv[m][k, t], reach)
+            bsend[m][k, t] = encode(pair, 2.0 * reach)
+            return c
+
+        lax.fori_loop(0, nz, one, 0)
+        for d in range(1, nz):
+            copy_b(m, k, d).start()
+
+    def phase_c(m, k):
+        for d in range(1, nz):
+            copy_b(m, k, d).wait_recv()
+        total = block(m, k, me) + decode(arecv[m][k, z], reach)
+        for d in range(1, nz):
+            total = total + decode(brecv[m][k, d - 1], 2.0 * reach)
+        master, memory = ((wu, wd)[m], (hu, hd)[m])
+        stepped, state = update(total, master[span(m, k), :], memory[span(m, k), :], rate)
+        (ou, od)[m][span(m, k), :] = stepped
+        (qu, qd)[m][span(m, k), :] = state
+        gath[m][me, span(m, k), :] = stepped.astype(jnp.bfloat16)
+        for d in range(1, nz):
+            copy_d(m, k, d).start()
+        copy_e(m, k, 0).start()
+        copy_out(m, k, 0).start()
+        copy_out(m, k, 1).start()
+
+    def phase_d(m, k):
+        for d in range(1, nz):
+            copy_d(m, k, d).wait_recv()
+            copy_e(m, k, d).start()
+
+    def phase_e(m, k):
+        for d in range(nz):
+            copy_e(m, k, d).wait_recv()
+        if m == 0:
+            copy_cu(k).start()
+        else:
+            for b in range(n):
+                copy_cd(k, b).start()
+
+    pl.semaphore_wait(barrier, n - 1)
+    each(0, phase_a)
+    each(1, phase_a)
+    for d in range(1, n):
+        copy_v(d).start()
+    each(0, phase_b)
+    each(1, phase_b)
+    for p in params:
+        p.wait()
+    each(0, phase_c)
+    each(1, phase_c)
+
+    for d in range(1, n):
+        copy_v(d).wait_recv()
+    slot = lambda j: lax.rem(me - j + n - 1 + n, n)
+    total = None
+    for j in range(n):
+        held = theirs[lax.rem(slot(j), n - 1)]
+        part = jnp.where(me == j, mine[...], held)
+        for i in range(4):
+            state_s[i * n + j : i * n + j + 1, :] = part[2 * n + i : 2 * n + i + 1, :]
+        total = part[0 : 2 * n, :] if total is None else total + part[0 : 2 * n, :]
+    stepped, state = update(total, state_s[0 : 2 * n, :], state_s[2 * n : 4 * n, :], rate)
+    cn[...] = stepped[0:n].astype(jnp.bfloat16)
+    cb[...] = stepped[n : 2 * n].astype(jnp.bfloat16)
+    step_s[0 : 2 * n, :] = stepped
+    state_s[0 : 2 * n, :] = state
+    tn[...] = step_s[pl.ds(me, 1), :]
+    tb[...] = step_s[pl.ds(me + n, 1), :]
+    vn[...] = state_s[pl.ds(me, 1), :]
+    vb[...] = state_s[pl.ds(me + n, 1), :]
+
+    each(0, phase_d)
+    each(1, phase_d)
+    each(0, phase_e)
+    each(1, phase_e)
+
+    def drain(m, k):
+        copy_a(m, k).wait_send()
+        for d in range(1, nz):
+            copy_b(m, k, d).wait_send()
+            copy_d(m, k, d).wait_send()
+        for d in range(nz):
+            copy_e(m, k, d).wait_send()
+        copy_out(m, k, 0).wait()
+        copy_out(m, k, 1).wait()
+        if m == 0:
+            copy_cu(k).wait()
+        else:
+            for b in range(n):
+                copy_cd(k, b).wait()
+
+    each(0, drain)
+    each(1, drain)
+    for d in range(1, n):
+        copy_v(d).wait_send()
+
+
+def fused(
+    n, partial_up, partial_down, partial_norm, partial_bias, master_up, master_down,
+    master_norm, master_bias, memory_up, memory_down, memory_norm, memory_bias,
+):
+    K = CHUNKS
+    nz = n // 2
+    hb, w = master_up.shape
+    rows, wide = master_down.shape
+    hr, rr = hb // K, rows // K
+    f32, b16 = jnp.float32, jnp.bfloat16
+    line = lambda a: a.reshape(1, -1)
+    operands = (
+        partial_up[0].reshape(n, hb, w), partial_down[0], master_up, master_down,
+        memory_up, memory_down, partial_norm.reshape(n, -1), partial_bias.reshape(n, -1),
+        line(master_norm), line(master_bias), line(memory_norm), line(memory_bias),
+    )
+    S = jax.ShapeDtypeStruct
+    shapes = (
+        S((n, hb, w), b16), S((rows, n * wide), b16),
+        S((hb, w), f32), S((rows, wide), f32), S((hb, w), f32), S((rows, wide), f32),
+        S((n, wide), b16), S((n, wide), b16),
+        S((1, wide), f32), S((1, wide), f32), S((1, wide), f32), S((1, wide), f32),
+    )
+    anyw = pl.BlockSpec(memory_space=pl.ANY)
+    vm = pl.BlockSpec(memory_space=pltpu.VMEM)
+    D = pltpu.SemaphoreType.DMA
+    V = pltpu.VMEM
+    cu, cd, tu, td, vu, vd, cn, cb, tn, tb, vn, vb = pl.pallas_call(
+        functools.partial(kernel, n),
+        out_shape=shapes,
+        in_specs=[anyw] * 6 + [vm] * 6,
+        out_specs=[anyw] * 6 + [vm] * 6,
+        scratch_shapes=[
+            V((n, hb, w), f32), V((rows, n * wide), f32),
+            V((hb, w), f32), V((rows, wide), f32), V((hb, w), f32), V((rows, wide), f32),
+            V((hb, w), f32), V((rows, wide), f32), V((hb, w), f32), V((rows, wide), f32),
+            V((K, nz, hr, w), b16), V((K, nz, rr, wide), b16),
+            V((K, nz, hr, w), b16), V((K, nz, rr, wide), b16),
+            V((K, nz, hr, w), b16), V((K, nz, rr, wide), b16),
+            V((K, nz - 1, hr, w), b16), V((K, nz - 1, rr, wide), b16),
+            V((n, hb, w), b16), V((n, rows, wide), b16),
+            V((2 * n + 8, wide), f32), V((n - 1, 2 * n + 8, wide), f32),
+            V((2 * n + 8, wide), f32), V((4 * n, wide), f32),
+            D((2, K)), D((4,)), D((2, K)), D((2, K)), D((2, K, nz - 1)), D((2, K, nz - 1)),
+            D((2, K, nz - 1)), D((2, K, nz - 1)), D((2, K, nz)), D((2, K, nz)),
+            D((n - 1,)), D((n - 1,)), D((2, K, 2)), D((K,)), D((K, n)),
+        ],
+        compiler_params=pltpu.CompilerParams(
+            collective_id=0, has_side_effects=True, vmem_limit_bytes=48 * 1024 * 1024
+        ),
+    )(*operands)
+    flat = lambda a: a.reshape(-1)
+    return (
+        cu.reshape(n * hb, w), cd, flat(cn), flat(cb),
+        tu, td, flat(tn), flat(tb), vu, vd, flat(vn), flat(vb),
+    )
+
+
+def on_device(*args):
+    n = lax.axis_size("replica")
+    hb, rows, wide = args[4].shape[0], args[5].shape[0], args[5].shape[1]
+    fits = n % 8 == 0 and wide == 128 and args[6].shape[0] == wide and args[7].shape[0] == wide
+    fits = fits and hb % (16 * CHUNKS) == 0 and rows % (16 * CHUNKS) == 0 and n <= 16
+    return fused(n, *args) if fits else plain(*args)
+
+
 def solution(mesh):
     in_specs = (
         P("replica", None, "model"),

time: 309 us -> 136 us (0.44)
  waiting for transfers between devices: 228 us -> 0 us
  Pallas kernels: 0 us -> 116 us
  blocking collectives: 55.8 us -> 0 us
  local copies, waits for them, and re-layouts: 4.6 us -> 19.1 us
  between operations: 13.9 us -> 0.69 us
  other arithmetic: 6.94 us -> 0 us
    reduce_scatter x2 -> x0, waiting for transfers between devices: 184 us -> none  [the longest x1 93.9 us: on_device(): lax.psum_scatter(partial_up[0], 'replica', scatter_dimension=0, tiled=True)]
    pallas_call x0 -> x1, Pallas kernels: none -> 116 us  [fused(): pl.pallas_call(functools.partial(kernel, n), out_shape=shapes, in_specs=[...]
    all_gather x2 -> x0, waiting for transfers between devices: 42.8 us -> none  [the longest x1 42.8 us: on_device(): lax.all_gather(stepped_down.astype(jnp.bfloat16), 'replica', axis=1, tile...]
    all_gather x2 -> x0, blocking collectives: 35.1 us -> none  [the longest x1 18.6 us: on_device(): lax.all_gather(stepped_bias.astype(jnp.bfloat16), 'replica', axis=0, tile...]
    psum x1 -> x0, blocking collectives: 20.6 us -> none  [on_device(): lax.psum((partial_norm[0], partial_bias[0]), 'replica')]
    unnamed x24 -> x34, local copies, waits for them, and re-layouts: 4.6 us -> 19.1 us
    convert_element_type x2 -> x0, other arithmetic: 4.54 us -> none  [the longest x1 2.27 us: on_device(): stepped_down.astype(jnp.bfloat16)]
  transfers between devices with their start and end apart: 4 -> 0, of which waited for: 3 -> 0; matrix products, arithmetic and copies ran while one was open for 2% -> 0% of each run, Pallas kernels for 0% -> 0%
where the time goes in v1:
time: 136 us
  Pallas kernels  116 us (85%)
  local copies, waits for them, and re-layouts  19.1 us (14%)
    pallas_call x1, Pallas kernels, fused(): pl.pallas_call(functools.partial(kernel, n), out_shape=shapes, in_specs=[...  116 us
    unnamed x34, local copies, waits for them, and re-layouts  19.1 us

profile of v1, /device:TPU:0, one launch (start us, length us, event | category | flops | bytes accessed | tf_op | source)
XLA Modules:
  0.0 135.9 jit_solution(17192560157676096199)
XLA Ops:
  0.6 0.0 copy-start
  0.7 1.0 copy-done
  1.7 0.0 copy-start.1
  1.7 1.0 copy-done.1
  2.7 0.0 copy-start.2
  2.7 1.0 copy-done.2
  3.8 0.0 copy-start.3
  3.8 1.0 copy-done.3
  4.8 0.0 copy-start.4
  4.8 0.7 copy-done.4
  5.5 0.0 copy-start.5
  5.5 0.7 copy-done.5
  6.2 0.0 copy-start.6
  6.2 0.7 copy-done.6
  6.8 0.0 copy-start.7
  6.9 0.7 copy-done.7
  7.5 0.0 copy-start.8
  7.5 0.7 copy-done.8
  8.2 0.0 copy-start.9
  8.2 0.7 copy-done.9
  8.8 116.2 %shard_map.211 = (bf16[8,128,1024]{2,1,0:T(8,128)(2,1)}, bf16[1024,1024]{1,0:T(8,128)(2,1)}, f32[128,1024]{1,0:T(8,128)S(1)}, f32[1024,128]{1,0:T(8,128)S(1)}, f...) custom-call(f32[8,128,1024]{2,1,0:T(8,128)} %bitcast.27, ...), custom_call_target="tpu_custom_call" | custom-call | tf_op jit(solution)/shard_map/pallas_call | solution.py:352
  125.0 0.0 copy-start.10
  125.0 3.2 %copy.36 = bf16[1024,1024]{1,0:T(8,128)(2,1)} copy(bf16[1024,1024]{1,0:T(8,128)(2,1)} %bitcast.29) | data formatting | bytes 4194304
  128.2 0.0 copy-done.10
  128.2 1.3 copy.37
  129.6 0.6 copy.38
  130.1 0.6 copy.39
  130.7 0.8 copy.40
  131.5 0.8 copy.41
  132.3 0.5 copy.42
  132.8 0.5 copy.43
  133.3 0.8 copy.44
  134.1 0.8 copy.45
  134.9 0.5 copy.46
  135.4 0.5 copy.47
Async XLA Ops:
  0.6 1.0 copy-start
  1.7 1.0 copy-start.1
  2.7 1.0 copy-start.2
  3.8 1.0 copy-start.3
  4.8 0.7 copy-start.4
  5.5 0.7 copy-start.5
  6.2 0.7 copy-start.6
  6.8 0.7 copy-start.7
  7.5 0.7 copy-start.8
  8.2 0.7 copy-start.9
  125.0 3.2 %copy-start.10 = (bf16[1024,1024]{1,0:T(8,128)(2,1)S(1)}, bf16[1024,1024]{1,0:T(8,128)(2,1)}, u32[]{:S(2)}) copy-start(bf16[1024,1024]{1,0:T(8,128)(2,1)} %get-tuple-element.49) | copy-start | bytes 6291460

commit v2 on v1

--- a/solution.py
+++ b/solution.py
@@ -73,7 +73,7 @@
     )
 
 
-CHUNKS = 4
+CHUNKS = 8
 STEEP = 32.0
 SPAN = 124.0
 POWER = 2.0 * SPAN / math.log1p(STEEP)
@@ -100,12 +100,12 @@
 def kernel(
     n,
     pu, pd, mu, md, su, sd, pn, pb, mn, mb, sn, sb,
-    cu, cd, tu, td, vu, vd, cn, cb, tn, tb, vn, vb,
-    xu, xd, wu, wd, hu, hd, ou, od, qu, qd,
-    au, ad, ru, rd, bu, bd, zu, zd, gu, gd,
-    mine, theirs, step_s, state_s,
-    sem_in, sem_par, sem_as, sem_ar, sem_bs, sem_br, sem_ds, sem_dr, sem_es, sem_er,
-    sem_vs, sem_vr, sem_o, sem_cu, sem_cd,
+    gu, gd, ou, od, qu, qd, cn, cb, step_s, state_s,
+    xu, xd, wu, wd, hu, hd,
+    au, ad, ru, rd, bu, bd, zu, zd,
+    mine, theirs, hold_s,
+    sem_in, sem_par, sem_vec, sem_as, sem_ar, sem_bs, sem_br, sem_ds, sem_dr, sem_es, sem_er,
+    sem_vs, sem_vr,
 ):
     K = CHUNKS
     nz = n // 2
@@ -172,17 +172,6 @@
     def copy_v(d):
         return remote(mine, theirs.at[d - 1], sem_vs.at[d - 1], sem_vr.at[d - 1], lax.rem(me + d, n))
 
-    def copy_out(m, k, j):
-        src = ((ou, od), (qu, qd))[j][m]
-        dst = ((tu, td), (vu, vd))[j][m]
-        return pltpu.make_async_copy(src.at[span(m, k), :], dst.at[span(m, k), :], sem_o.at[m, k, j])
-
-    def copy_cu(k):
-        return pltpu.make_async_copy(gu.at[:, rows(k, hr), :], cu.at[:, rows(k, hr), :], sem_cu.at[k])
-
-    def copy_cd(k, b):
-        return pltpu.make_async_copy(gd.at[b, rows(k, rr), :], cd.at[rows(k, rr), lanes(b)], sem_cd.at[k, b])
-
     def each(m, body):
         lax.fori_loop(0, K, lambda k, c: (body(m, k), c)[1], 0)
 
@@ -195,11 +184,15 @@
     for p in params:
         p.start()
 
-    mine[0:n, :] = pn[...]
-    mine[n : 2 * n, :] = pb[...]
-    for i, a in enumerate((mn, mb, sn, sb)):
-        mine[2 * n + i : 2 * n + i + 1, :] = a[...]
+    vectors = [
+        pltpu.make_async_copy(a, mine.at[at : at + a.shape[0], :], sem_vec.at[i])
+        for i, (a, at) in enumerate(
+            ((pn, 0), (pb, n), (mn, 2 * n), (mb, 2 * n + 1), (sn, 2 * n + 2), (sb, 2 * n + 3))
+        )
+    ]
     mine[2 * n + 4 : 2 * n + 8, :] = jnp.zeros((4, wide), jnp.float32)
+    for p in vectors:
+        p.start()
 
     barrier = pltpu.get_barrier_semaphore()
     for d in range(1, n):
@@ -247,8 +240,6 @@
         for d in range(1, nz):
             copy_d(m, k, d).start()
         copy_e(m, k, 0).start()
-        copy_out(m, k, 0).start()
-        copy_out(m, k, 1).start()
 
     def phase_d(m, k):
         for d in range(1, nz):
@@ -258,15 +249,12 @@
     def phase_e(m, k):
         for d in range(nz):
             copy_e(m, k, d).wait_recv()
-        if m == 0:
-            copy_cu(k).start()
-        else:
-            for b in range(n):
-                copy_cd(k, b).start()
 
     pl.semaphore_wait(barrier, n - 1)
     each(0, phase_a)
     each(1, phase_a)
+    for p in vectors:
+        p.wait()
     for d in range(1, n):
         copy_v(d).start()
     each(0, phase_b)
@@ -284,17 +272,13 @@
         held = theirs[lax.rem(slot(j), n - 1)]
         part = jnp.where(me == j, mine[...], held)
         for i in range(4):
-            state_s[i * n + j : i * n + j + 1, :] = part[2 * n + i : 2 * n + i + 1, :]
+            hold_s[i * n + j : i * n + j + 1, :] = part[2 * n + i : 2 * n + i + 1, :]
         total = part[0 : 2 * n, :] if total is None else total + part[0 : 2 * n, :]
-    stepped, state = update(total, state_s[0 : 2 * n, :], state_s[2 * n : 4 * n, :], rate)
+    stepped, state = update(total, hold_s[0 : 2 * n, :], hold_s[2 * n : 4 * n, :], rate)
     cn[...] = stepped[0:n].astype(jnp.bfloat16)
     cb[...] = stepped[n : 2 * n].astype(jnp.bfloat16)
-    step_s[0 : 2 * n, :] = stepped
-    state_s[0 : 2 * n, :] = state
-    tn[...] = step_s[pl.ds(me, 1), :]
-    tb[...] = step_s[pl.ds(me + n, 1), :]
-    vn[...] = state_s[pl.ds(me, 1), :]
-    vb[...] = state_s[pl.ds(me + n, 1), :]
+    step_s[...] = stepped
+    state_s[...] = state
 
     each(0, phase_d)
     each(1, phase_d)
@@ -308,18 +292,29 @@
             copy_d(m, k, d).wait_send()
         for d in range(nz):
             copy_e(m, k, d).wait_send()
-        copy_out(m, k, 0).wait()
-        copy_out(m, k, 1).wait()
-        if m == 0:
-            copy_cu(k).wait()
-        else:
-            for b in range(n):
-                copy_cd(k, b).wait()
 
     each(0, drain)
     each(1, drain)
     for d in range(1, n):
         copy_v(d).wait_send()
+
+
+def leave(
+    n, gu, gd, ou, od, qu, qd, cn, cb, step_s, state_s,
+    cu, cd, tu, td, vu, vd, xcn, xcb, tn, tb, vn, vb, sem,
+):
+    me = lax.axis_index("replica")
+    wide = gd.shape[2]
+    pairs = [(gu, cu)]
+    pairs += [(gd.at[b], cd.at[:, b * wide : (b + 1) * wide]) for b in range(n)]
+    pairs += [(ou, tu), (od, td), (qu, vu), (qd, vd), (cn, xcn), (cb, xcb)]
+    pairs += [(step_s.at[pl.ds(me, 1), :], tn), (step_s.at[pl.ds(me + n, 1), :], tb)]
+    pairs += [(state_s.at[pl.ds(me, 1), :], vn), (state_s.at[pl.ds(me + n, 1), :], vb)]
+    copies = [pltpu.make_async_copy(a, b, sem.at[i]) for i, (a, b) in enumerate(pairs)]
+    for c in copies:
+        c.start()
+    for c in copies:
+        c.wait()
 
 
 def fused(
@@ -345,34 +340,43 @@
         S((n, wide), b16), S((n, wide), b16),
         S((1, wide), f32), S((1, wide), f32), S((1, wide), f32), S((1, wide), f32),
     )
-    anyw = pl.BlockSpec(memory_space=pl.ANY)
+    hbm = pl.BlockSpec(memory_space=pltpu.HBM)
     vm = pl.BlockSpec(memory_space=pltpu.VMEM)
     D = pltpu.SemaphoreType.DMA
     V = pltpu.VMEM
-    cu, cd, tu, td, vu, vd, cn, cb, tn, tb, vn, vb = pl.pallas_call(
+    held = pl.pallas_call(
         functools.partial(kernel, n),
-        out_shape=shapes,
-        in_specs=[anyw] * 6 + [vm] * 6,
-        out_specs=[anyw] * 6 + [vm] * 6,
+        out_shape=(
+            S((n, hb, w), b16), S((n, rows, wide), b16),
+            S((hb, w), f32), S((rows, wide), f32), S((hb, w), f32), S((rows, wide), f32),
+            S((n, wide), b16), S((n, wide), b16), S((2 * n, wide), f32), S((2 * n, wide), f32),
+        ),
+        in_specs=[hbm] * 12,
+        out_specs=[vm] * 10,
         scratch_shapes=[
             V((n, hb, w), f32), V((rows, n * wide), f32),
-            V((hb, w), f32), V((rows, wide), f32), V((hb, w), f32), V((rows, wide), f32),
             V((hb, w), f32), V((rows, wide), f32), V((hb, w), f32), V((rows, wide), f32),
             V((K, nz, hr, w), b16), V((K, nz, rr, wide), b16),
             V((K, nz, hr, w), b16), V((K, nz, rr, wide), b16),
             V((K, nz, hr, w), b16), V((K, nz, rr, wide), b16),
             V((K, nz - 1, hr, w), b16), V((K, nz - 1, rr, wide), b16),
-            V((n, hb, w), b16), V((n, rows, wide), b16),
-            V((2 * n + 8, wide), f32), V((n - 1, 2 * n + 8, wide), f32),
-            V((2 * n + 8, wide), f32), V((4 * n, wide), f32),
-            D((2, K)), D((4,)), D((2, K)), D((2, K)), D((2, K, nz - 1)), D((2, K, nz - 1)),
-            D((2, K, nz - 1)), D((2, K, nz - 1)), D((2, K, nz)), D((2, K, nz)),
-            D((n - 1,)), D((n - 1,)), D((2, K, 2)), D((K,)), D((K, n)),
+            V((2 * n + 8, wide), f32), V((n - 1, 2 * n + 8, wide), f32), V((4 * n, wide), f32),
+            D((2, K)), D((4,)), D((6,)), D((2, K)), D((2, K)), D((2, K, nz - 1)),
+            D((2, K, nz - 1)), D((2, K, nz - 1)), D((2, K, nz - 1)), D((2, K, nz)),
+            D((2, K, nz)), D((n - 1,)), D((n - 1,)),
         ],
         compiler_params=pltpu.CompilerParams(
-            collective_id=0, has_side_effects=True, vmem_limit_bytes=48 * 1024 * 1024
+            collective_id=0, has_side_effects=True, vmem_limit_bytes=40 * 1024 * 1024
         ),
-    )(*operands)
+    )(*[pltpu.with_memory_space_constraint(a, pltpu.HBM) for a in operands])
+    cu, cd, tu, td, vu, vd, cn, cb, tn, tb, vn, vb = pl.pallas_call(
+        functools.partial(leave, n),
+        out_shape=shapes,
+        in_specs=[vm] * 10,
+        out_specs=[hbm] * 12,
+        scratch_shapes=[D((n + 11,))],
+        compiler_params=pltpu.CompilerParams(vmem_limit_bytes=4 * 1024 * 1024),
+    )(*held)
     flat = lambda a: a.reshape(-1)
     return (
         cu.reshape(n * hb, w), cd, flat(cn), flat(cb),

time: 136 us -> 119 us (0.88)
  local copies, waits for them, and re-layouts: 19.1 us -> 0 us
  Pallas kernels: 116 us -> 118 us
    unnamed x34 -> x0, local copies, waits for them, and re-layouts: 19.1 us -> none
    pallas_call x1 -> x2, Pallas kernels: 116 us -> 118 us  [the longest x1 115 us: fused(): pl.pallas_call(functools.partial(kernel, n), out_shape=(S((n, hb, w), b16...]
where the time goes in v2:
time: 119 us
  Pallas kernels  118 us (99%)
    pallas_call x1, Pallas kernels, fused(): pl.pallas_call(functools.partial(kernel, n), out_shape=(S((n, hb, w), b16...  115 us
    pallas_call x1, Pallas kernels, fused(): pl.pallas_call(functools.partial(leave, n), out_shape=shapes, in_specs=[v...  2.83 us

profile of v2, /device:TPU:0, one launch (start us, length us, event | category | flops | bytes accessed | tf_op | source)
XLA Modules:
  0.0 118.8 jit_solution(3602171067888387929)
XLA Ops:
  0.6 115.3 %shard_map.211 = (bf16[8,128,1024]{2,1,0:T(8,128)(2,1)S(1)}, bf16[8,1024,128]{2,1,0:T(8,128)(2,1)S(1)}, f32[128,1024]{1,0:T(8,128)S(1)}, f32[1024,128]{1,0:T(8,1...) custom-call(f32[8,128,1024]{2,1,0:T(8,128)} %bitcast.15, ...), custom_call_target="tpu_custom_call" | custom-call | tf_op jit(solution)/shard_map/pallas_call | solution.py:347
  115.9 2.8 %shard_map.212 = (bf16[8,128,1024]{2,1,0:T(8,128)(2,1)}, bf16[1024,1024]{1,0:T(8,128)(2,1)}, f32[128,1024]{1,0:T(8,128)}, f32[1024,128]{1,0:T(8,128)}, f32[128,1...) custom-call(bf16[8,128,1024]{2,1,0:T(8,128)(2,1)S(1)} %get-tuple-ele, ...), custom_call_target="tpu_custom_call" | custom-call | tf_op jit(solution)/shard_map/pallas_call | solution.py:372

commit v3 on v2

--- a/solution.py
+++ b/solution.py
@@ -161,13 +161,27 @@
             sem_bs.at[m, k, d - 1], sem_br.at[m, k, d - 1], 2 * up_z(d) + y,
         )
 
-    def copy_d(m, k, d):
-        piece = gath[m].at[me, span(m, k), :]
-        return remote(piece, piece, sem_ds.at[m, k, d - 1], sem_dr.at[m, k, d - 1], 2 * up_z(d) + y)
-
-    def copy_e(m, k, d):
-        piece = gath[m].at[2 * from_z(d) + y, span(m, k), :]
-        return remote(piece, piece, sem_es.at[m, k, d], sem_er.at[m, k, d], other)
+    def inside(t):
+        return jnp.logical_and(t >= 0, t < nz)
+
+    def copy_d(m, k, way, d):
+        step = (1, -1)[way]
+        piece = gath[m].at[2 * (z - step * d) + y, span(m, k), :]
+        at = way * (nz - 1) + d
+        return remote(piece, piece, sem_ds.at[m, k, at], sem_dr.at[m, k, at], 2 * (z + step) + y)
+
+    def landed_d(m, k, way, d):
+        piece = gath[m].at[2 * (z - (1, -1)[way] * d) + y, span(m, k), :]
+        at = way * (nz - 1) + d - 1
+        return remote(piece, piece, sem_ds.at[m, k, at], sem_dr.at[m, k, at], other)
+
+    def sends(way, d):
+        step = (1, -1)[way]
+        return jnp.logical_and(inside(z - step * d), inside(z + step))
+
+    def copy_e(m, k, t):
+        piece = gath[m].at[2 * t + y, span(m, k), :]
+        return remote(piece, piece, sem_es.at[m, k, t], sem_er.at[m, k, t], other)
 
     def copy_v(d):
         return remote(mine, theirs.at[d - 1], sem_vs.at[d - 1], sem_vr.at[d - 1], lax.rem(me + d, n))
@@ -237,14 +251,28 @@
         (ou, od)[m][span(m, k), :] = stepped
         (qu, qd)[m][span(m, k), :] = state
         gath[m][me, span(m, k), :] = stepped.astype(jnp.bfloat16)
-        for d in range(1, nz):
-            copy_d(m, k, d).start()
-        copy_e(m, k, 0).start()
-
-    def phase_d(m, k):
-        for d in range(1, nz):
-            copy_d(m, k, d).wait_recv()
-            copy_e(m, k, d).start()
+        copy_e(m, k, z).start()
+        for way in range(2):
+
+            @pl.when(sends(way, 0))
+            def _():
+                copy_d(m, k, way, 0).start()
+
+
+    def phase_d(m, k, d):
+        for way in range(2):
+            origin = z - (1, -1)[way] * d
+
+            @pl.when(inside(origin))
+            def _():
+                landed_d(m, k, way, d).wait_recv()
+                copy_e(m, k, origin).start()
+
+            if d < nz - 1:
+
+                @pl.when(sends(way, d))
+                def _():
+                    copy_d(m, k, way, d).start()
 
     def phase_e(m, k):
         for d in range(nz):
@@ -258,10 +286,14 @@
     for d in range(1, n):
         copy_v(d).start()
     each(0, phase_b)
-    each(1, phase_b)
     for p in params:
         p.wait()
-    each(0, phase_c)
+
+    def phase_bc(m, k):
+        phase_b(1, k)
+        phase_c(0, k)
+
+    each(0, phase_bc)
     each(1, phase_c)
 
     for d in range(1, n):
@@ -280,8 +312,9 @@
     step_s[...] = stepped
     state_s[...] = state
 
-    each(0, phase_d)
-    each(1, phase_d)
+    for d in range(1, nz):
+        each(0, functools.partial(phase_d, d=d))
+        each(1, functools.partial(phase_d, d=d))
     each(0, phase_e)
     each(1, phase_e)
 
@@ -289,7 +322,12 @@
         copy_a(m, k).wait_send()
         for d in range(1, nz):
             copy_b(m, k, d).wait_send()
-            copy_d(m, k, d).wait_send()
+            for way in range(2):
+
+                @pl.when(sends(way, d - 1))
+                def _():
+                    copy_d(m, k, way, d - 1).wait_send()
+
         for d in range(nz):
             copy_e(m, k, d).wait_send()
 
@@ -362,7 +400,7 @@
             V((K, nz - 1, hr, w), b16), V((K, nz - 1, rr, wide), b16),
             V((2 * n + 8, wide), f32), V((n - 1, 2 * n + 8, wide), f32), V((4 * n, wide), f32),
             D((2, K)), D((4,)), D((6,)), D((2, K)), D((2, K)), D((2, K, nz - 1)),
-            D((2, K, nz - 1)), D((2, K, nz - 1)), D((2, K, nz - 1)), D((2, K, nz)),
+            D((2, K, nz - 1)), D((2, K, 2 * nz - 2)), D((2, K, 2 * nz - 2)), D((2, K, nz)),
             D((2, K, nz)), D((n - 1,)), D((n - 1,)),
         ],
         compiler_params=pltpu.CompilerParams(

time: 119 us -> 107 us (0.90)
  Pallas kernels: 118 us -> 106 us
    pallas_call x1, Pallas kernels: 115 us -> 103 us  [fused(): pl.pallas_call(functools.partial(kernel, n), out_shape=(S((n, hb, w), b16...]
where the time goes in v3:
time: 107 us
  Pallas kernels  106 us (99%)
    pallas_call x1, Pallas kernels, fused(): pl.pallas_call(functools.partial(kernel, n), out_shape=(S((n, hb, w), b16...  103 us
    pallas_call x1, Pallas kernels, fused(): pl.pallas_call(functools.partial(leave, n), out_shape=shapes, in_specs=[v...  2.83 us

profile of v3, /device:TPU:0, one launch (start us, length us, event | category | flops | bytes accessed | tf_op | source)
XLA Modules:
  0.0 106.8 jit_solution(15277209894088173625)
XLA Ops:
  0.6 103.3 %shard_map.211 = (bf16[8,128,1024]{2,1,0:T(8,128)(2,1)S(1)}, bf16[8,1024,128]{2,1,0:T(8,128)(2,1)S(1)}, f32[128,1024]{1,0:T(8,128)S(1)}, f32[1024,128]{1,0:T(8,1...) custom-call(f32[8,128,1024]{2,1,0:T(8,128)} %bitcast.15, ...), custom_call_target="tpu_custom_call" | custom-call | tf_op jit(solution)/shard_map/pallas_call | solution.py:385
  103.9 2.8 %shard_map.212 = (bf16[8,128,1024]{2,1,0:T(8,128)(2,1)}, bf16[1024,1024]{1,0:T(8,128)(2,1)}, f32[128,1024]{1,0:T(8,128)}, f32[1024,128]{1,0:T(8,128)}, f32[128,1...) custom-call(bf16[8,128,1024]{2,1,0:T(8,128)(2,1)S(1)} %get-tuple-ele, ...), custom_call_target="tpu_custom_call" | custom-call | tf_op jit(solution)/shard_map/pallas_call | solution.py:410
